TPU v7x, 32 devices: a whole 2x2x4 slice. The times are simulated.
32 devices in a mesh: group: 2 (over x), seq: 8 (over z, y), head: 2 (over core).
Axes of the slice: x: 2, y: 2, z: 4, core: 2. Of those that a mesh axis runs over, the one named last changes fastest.
Arguments:
- queries: bfloat16 [4096, 8192], P(('group', 'seq', 'head')), parts along dimension 0, may hold values from -6 to 6
- keys: bfloat16 [4096, 1024], P(('group', 'seq', 'head')), parts along dimension 0, may hold values from -6 to 6
- values: bfloat16 [4096, 1024], P(('group', 'seq', 'head')), parts along dimension 0, may hold values from -6 to 6
- lengths: int32 [8], P('group'), parts along dimension 0, may hold values from 1 to 1024, 2048 in all
- assign: int32 [32], P('group'), parts along dimension 0, may hold values from 0 to 15, each once
Outputs:
- attended: bfloat16 [4096, 8192], P(('group', 'seq', 'head')), parts along dimension 0
There are 2 independent parts, one for each index of `group`. A program takes and returns all parts, laid end to end along the dimension named above; each array names one. Nothing has to cross between parts.
Inputs may be any that keep to these rules, and one draw needn't show every extreme that they name: 4 positive lengths summing to 2048, the largest exactly 1024. `assign`: each span index once.
All inputs are finite; a program needn't handle non-finite values.
Results may differ from a plain program's by a relative error of at most 0.004.
Values may be sent and summed in bfloat16 or wider, within the bound.
A program may use at most 128 MiB of HBM per device.

v0:
```python
import math

import jax
import jax.numpy as jnp
from jax import lax
from jax.sharding import PartitionSpec as P

QUERY_HEADS = 64
KEY_VALUE_HEADS = 8
HEAD_SIZE = 128


def token_places(rows, assign, ends, span):
    span_of = rows // span
    table = jnp.arange(assign.shape[0], dtype=jnp.int32)
    picked = jnp.sum(jnp.where(span_of[:, None] == table[None, :], assign[None, :], 0), axis=1)
    place = picked * span + rows % span
    owner = jnp.sum((place[:, None] >= ends[None, :]).astype(jnp.int32), axis=1)
    return (place, owner)


def attend_block(carry, grouped, q_place, q_doc, key_block, value_block, k_place, k_doc):
    visible = (q_doc[:, None] == k_doc[None, :]) & (k_place[None, :] <= q_place[:, None])
    scale = 1.0 / math.sqrt(HEAD_SIZE)

    def compute(state):
        running, total, accum = state
        scores = (
            jnp.einsum("rkgd,pkd->kgrp", grouped, key_block, preferred_element_type=jnp.float32)
            * scale
        )
        scores = jnp.where(visible, scores, -1e30)
        highest = jnp.maximum(running, jnp.max(scores, axis=-1))
        weights = jnp.where(visible, jnp.exp(scores - highest[..., None]), 0.0)
        factor = jnp.exp(running - highest)
        total = total * factor + jnp.sum(weights, axis=-1)
        accum = accum * factor[..., None] + jnp.einsum(
            "kgrp,pkd->kgrd",
            weights.astype(jnp.bfloat16),
            value_block,
            preferred_element_type=jnp.float32,
        )
        return (highest, total, accum)

    def keep(state):
        return state

    return lax.cond(jnp.any(visible), compute, keep, carry)


def make_folder(grouped, q_place, q_doc, kv_heads, assign, ends, span):

    def folder(carry, pieces, start):
        key_rows, value_rows = pieces
        count = key_rows.shape[0]
        width = math.gcd(count, 512)
        turns = count // width

        def advance(index, state):
            offset = index * width
            key_block = lax.dynamic_slice_in_dim(key_rows, offset, width, 0).reshape(
                width, kv_heads, HEAD_SIZE
            )
            value_block = lax.dynamic_slice_in_dim(value_rows, offset, width, 0).reshape(
                width, kv_heads, HEAD_SIZE
            )
            rows = offset + jnp.arange(width, dtype=jnp.int32)
            k_place, k_doc = token_places(rows, assign, ends, span)
            return attend_block(
                state, grouped, q_place, q_doc, key_block, value_block, k_place, k_doc
            )

        return lax.fori_loop(0, turns, advance, carry)

    return folder


def prepare(queries, first, kv_heads, assign, ends, span):
    count = queries.shape[0]
    query_group = QUERY_HEADS // KEY_VALUE_HEADS
    grouped = queries.reshape(count, kv_heads, query_group, HEAD_SIZE)
    rows = jnp.asarray(first) + jnp.arange(count, dtype=jnp.int32)
    q_place, q_doc = token_places(rows, assign, ends, span)
    start_state = (
        jnp.full((kv_heads, query_group, count), -1e30, jnp.float32),
        jnp.zeros((kv_heads, query_group, count), jnp.float32),
        jnp.zeros((kv_heads, query_group, count, HEAD_SIZE), jnp.float32),
    )
    folder = make_folder(grouped, q_place, q_doc, kv_heads, assign, ends, span)
    return (folder, start_state)


def finish(state):
    running, total, accum = state
    result = accum / total[..., None]
    kv_heads, query_group, count, width = result.shape
    return (
        result.transpose(2, 0, 1, 3)
        .reshape(count, kv_heads * query_group * width)
        .astype(jnp.bfloat16)
    )


def local(queries, keys, values, lengths, assign):
    span = queries.shape[0]
    ends = jnp.cumsum(lengths)
    kv_heads = keys.shape[1] // HEAD_SIZE
    first = lax.axis_index(("seq", "head")) * span
    folder, start_state = prepare(queries, first, kv_heads, assign, ends, span)
    state = folder(
        start_state,
        (
            lax.all_gather(keys, ("seq", "head"), axis=0, tiled=True),
            lax.all_gather(values, ("seq", "head"), axis=0, tiled=True),
        ),
        jnp.int32(0),
    )
    return finish(state)


def solution(mesh):
    placed = (
        P(("group", "seq", "head"), None),
        P(("group", "seq", "head"), None),
        P(("group", "seq", "head"), None),
        P("group"),
        P("group"),
    )
    return jax.shard_map(
        local,
        mesh=mesh,
        in_specs=placed,
        out_specs=P(("group", "seq", "head"), None),
        check_vma=False,
    )
```

profile of v0, /device:TPU:13, one launch (start us, length us, event | category | flops | bytes accessed | tf_op | source)
XLA Modules:
  0.0 212.4 jit_solution(269422098565435676)
XLA Ops:
  6.5 1.8 copy.19
  8.3 0.0 all-gather.3.cloned.1.call-update
  8.4 0.0 all-gather.5.cloned.1.call-start
  8.4 1.8 copy.21
  10.3 3.2 %copy.20 = bf16[128,8192]{0,1:T(8,128)(2,1)S(1)} copy(bf16[128,8192]{1,0:T(8,128)(2,1)} %param.9) | data formatting | bytes 4194304 | tf_op args[0]
  13.5 2.6 %copy.22 = bf16[128,8,8,128]{3,0,2,1:T(8,128)(2,1)} copy(bf16[128,8,8,128]{0,3,2,1:T(8,128)(2,1)S(1)} %bitcast.39) | data formatting | bytes 4194304 | tf_op jit(solution)/shard_map/while | solution.py:73
  16.1 0.2 reduce-window.8
  16.3 0.1 select_reduce_fusion.1
  16.4 0.1 convert_reduce_fusion.1
  16.5 44.4 %all-gather.3.cloned.1.call-done = bf16[2048,1024]{0,1:T(8,128)(2,1)} async-done(((bf16[128,1024]{0,1:T(8,128)(2,1)}), bf16[2048,1024]{0,1:T(8,128)(2,1)}) %all-gather.3.cloned.1.call-update) | async-done | bytes 4194320 | tf_op jit(solution)/shard_map/all_gather | solution.py:113
  60.9 52.8 %all-gather.5.cloned.1.call-done = bf16[2048,1024]{0,1:T(8,128)(2,1)} async-done(((bf16[128,1024]{0,1:T(8,128)(2,1)}), bf16[2048,1024]{0,1:T(8,128)(2,1)}) %all-gather.5.cloned.1.call-update) | async-done | bytes 4194320 | tf_op jit(solution)/shard_map/all_gather | solution.py:114
  113.7 2.5 %broadcast_in_dim.109 = f32[8,8,128,128]{3,2,1,0:T(8,128)} broadcast(f32[]{:T(128)} %constant.175.clone.1), dimensions={} | broadcast | bytes 4194308 | tf_op jit(solution)/shard_map/broadcast_in_dim | solution.py:87
  116.2 82.0 %while.19 = (s32[]{:T(128)}, f32[8,8,128]{2,1,0:T(8,128)S(1)}, f32[8,8,128]{2,1,0:T(8,128)S(1)}, f32[8,8,128,128]{3,2,1,0:T(8,128)}, s32[128]{0:T(128)S(1)}, /*i...) while((s32[]{:T(128)}, f32[8,8,128]{2,1,0:T(8,128)S(1)}, ...), condition=%wide.region_11.12_spmd, body=%wide.region_3.11_spmd.sunk | while | flops 2204430336 | bytes 76303776 | solution.py:73
  116.2 0.1 select_reduce_fusion.3
  116.3 0.1 convert_reduce_fusion.3
  116.4 0.9 fusion.24
  117.9 18.8 %conditional.2 = ((f32[8,8,128]{2,1,0:T(8,128)S(1)}, f32[8,8,128]{2,1,0:T(8,128)S(1)}, f32[8,8,128,128]{3,2,1,0:T(8,128)})) conditional(s32[]{:T(128)} %convert_element_type.54, (f32[8,8,128]{2,1,0:T(8,128)S(1)}, f32[8,8,128]{2,1,0:T(8,128)S(1)}, f32[8,8,128,128]{3,2,1,0:T(8,128)}) %tuple.62, (pred[128,512]{0,1:T(8,128)(4,1)S(1)}, s32[]{:T(128)}, ...), branch_computations={%region_7.7_spmd, %region_8.10_spmd} | conditional | flops 2204123136 | bytes 76218464 | solution.py:48
  117.9 2.9 %constant_dynamic-slice_fusion = (bf16[512,1024]{0,1:T(8,128)(2,1)}, bf16[512,1024]{0,1:T(8,128)(2,1)S(1)}) fusion(bf16[2048,1024]{0,1:T(8,128)(2,1)} %get-tuple-element.375, s32[]{:T(128)S(6)} %select_n.100, bf16[2048,1024]{0,1:T(8,128)(2,1)} %get-tuple-element.370), kind=kLoop, calls=%fused_computation.10 | loop fusion | bytes 4194308 | tf_op jit(solution)/shard_map/while/body/eval_jaxpr/dynamic_slice | solution.py:64
  120.8 2.7 %fusion = (f32[8,8,128]{2,1,0:T(8,128)S(1)}, f32[8,512,128,8]{2,1,3,0:T(8,128)S(1)}) fusion(pred[128,512]{0,1:T(8,128)(4,1)S(1)} %get-tuple-element.369, bf16[512,8,128,1]{0,2,3,1:T(8,128)(2,1)S(1)} %bitcast.36, bf16[128,8,8,128]{3,0,2,1:T(8,128)(2,1)S(1)} %copy-done), kind=kOutput, calls=%fused_computation.2 | convolution fusion | flops 1086316544 | bytes 20021248 | tf_op jit(solution)/shard_map/while/body/eval_jaxpr/cond/branch_1_fun/rkgd,pkd->kgrp/dot_general | solution.py:29
  123.5 4.2 %fusion.2 = f32[8,8,128]{2,1,0:T(8,128)S(1)} fusion(f32[8,512,128,8]{2,1,3,0:T(8,128)S(1)} %get-tuple-element.444, f32[8,8,128]{2,1,0:T(8,128)S(1)} %max.5, pred[128,512]{0,1:T(8,128)(4,1)S(1)} %get-tuple-element.369), kind=kLoop, calls=%fused_computation.4 | loop fusion | flops 20963328 | bytes 16908288 | tf_op jit(solution)/shard_map/while/body/eval_jaxpr/cond/branch_1_fun/reduce_sum | solution.py:36
  127.8 8.9 %multiply_add_fusion = f32[8,8,128,128]{3,2,1,0:T(8,128)} fusion(f32[8,8,128,128]{3,2,1,0:T(8,128)} %get-tuple-element.374, f32[8,8,128]{2,1,0:T(8,128)S(1)} %get-tuple-element.440, bf16[512,8,128,1]{0,2,3,1:T(8,128)(2,1)} %bitcast.37, f32[8,512,128,8]{2,1,3,0:T(8,128)S(1)} %get-tuple-element.444, f32[8,8,128]{2,1,0:T(8,128)S(1)} %max.5, ...), kind=kOutput, calls=%fused_computation.7 | convolution fusion | flops 1096810496 | bytes 26345472 | tf_op jit(solution)/shard_map/while/body/eval_jaxpr/cond/branch_1_fun/kgrp,pkd->kgrd/dot_general | solution.py:37
  136.7 0.1 select_reduce_fusion.3
  136.8 0.1 convert_reduce_fusion.3
  136.9 0.9 fusion.24
  138.4 18.8 %conditional.2 = ((f32[8,8,128]{2,1,0:T(8,128)S(1)}, f32[8,8,128]{2,1,0:T(8,128)S(1)}, f32[8,8,128,128]{3,2,1,0:T(8,128)})) conditional(s32[]{:T(128)} %convert_element_type.54, (f32[8,8,128]{2,1,0:T(8,128)S(1)}, f32[8,8,128]{2,1,0:T(8,128)S(1)}, f32[8,8,128,128]{3,2,1,0:T(8,128)}) %tuple.62, (pred[128,512]{0,1:T(8,128)(4,1)S(1)}, s32[]{:T(128)}, ...), branch_computations={%region_7.7_spmd, %region_8.10_spmd} | conditional | flops 2204123136 | bytes 76218464 | solution.py:48
  138.4 2.9 %constant_dynamic-slice_fusion = (bf16[512,1024]{0,1:T(8,128)(2,1)}, bf16[512,1024]{0,1:T(8,128)(2,1)S(1)}) fusion(bf16[2048,1024]{0,1:T(8,128)(2,1)} %get-tuple-element.375, s32[]{:T(128)S(6)} %select_n.100, bf16[2048,1024]{0,1:T(8,128)(2,1)} %get-tuple-element.370), kind=kLoop, calls=%fused_computation.10 | loop fusion | bytes 4194308 | tf_op jit(solution)/shard_map/while/body/eval_jaxpr/dynamic_slice | solution.py:64
  141.3 2.7 %fusion = (f32[8,8,128]{2,1,0:T(8,128)S(1)}, f32[8,512,128,8]{2,1,3,0:T(8,128)S(1)}) fusion(pred[128,512]{0,1:T(8,128)(4,1)S(1)} %get-tuple-element.369, bf16[512,8,128,1]{0,2,3,1:T(8,128)(2,1)S(1)} %bitcast.36, bf16[128,8,8,128]{3,0,2,1:T(8,128)(2,1)S(1)} %copy-done), kind=kOutput, calls=%fused_computation.2 | convolution fusion | flops 1086316544 | bytes 20021248 | tf_op jit(solution)/shard_map/while/body/eval_jaxpr/cond/branch_1_fun/rkgd,pkd->kgrp/dot_general | solution.py:29
  144.0 4.2 %fusion.2 = f32[8,8,128]{2,1,0:T(8,128)S(1)} fusion(f32[8,512,128,8]{2,1,3,0:T(8,128)S(1)} %get-tuple-element.444, f32[8,8,128]{2,1,0:T(8,128)S(1)} %max.5, pred[128,512]{0,1:T(8,128)(4,1)S(1)} %get-tuple-element.369), kind=kLoop, calls=%fused_computation.4 | loop fusion | flops 20963328 | bytes 16908288 | tf_op jit(solution)/shard_map/while/body/eval_jaxpr/cond/branch_1_fun/reduce_sum | solution.py:36
  148.3 8.9 %multiply_add_fusion = f32[8,8,128,128]{3,2,1,0:T(8,128)} fusion(f32[8,8,128,128]{3,2,1,0:T(8,128)} %get-tuple-element.374, f32[8,8,128]{2,1,0:T(8,128)S(1)} %get-tuple-element.440, bf16[512,8,128,1]{0,2,3,1:T(8,128)(2,1)} %bitcast.37, f32[8,512,128,8]{2,1,3,0:T(8,128)S(1)} %get-tuple-element.444, f32[8,8,128]{2,1,0:T(8,128)S(1)} %max.5, ...), kind=kOutput, calls=%fused_computation.7 | convolution fusion | flops 1096810496 | bytes 26345472 | tf_op jit(solution)/shard_map/while/body/eval_jaxpr/cond/branch_1_fun/kgrp,pkd->kgrd/dot_general | solution.py:37
  157.2 0.1 select_reduce_fusion.3
  157.3 0.1 convert_reduce_fusion.3
  157.4 0.9 fusion.24
  158.9 18.8 %conditional.2 = ((f32[8,8,128]{2,1,0:T(8,128)S(1)}, f32[8,8,128]{2,1,0:T(8,128)S(1)}, f32[8,8,128,128]{3,2,1,0:T(8,128)})) conditional(s32[]{:T(128)} %convert_element_type.54, (f32[8,8,128]{2,1,0:T(8,128)S(1)}, f32[8,8,128]{2,1,0:T(8,128)S(1)}, f32[8,8,128,128]{3,2,1,0:T(8,128)}) %tuple.62, (pred[128,512]{0,1:T(8,128)(4,1)S(1)}, s32[]{:T(128)}, ...), branch_computations={%region_7.7_spmd, %region_8.10_spmd} | conditional | flops 2204123136 | bytes 76218464 | solution.py:48
  158.9 2.9 %constant_dynamic-slice_fusion = (bf16[512,1024]{0,1:T(8,128)(2,1)}, bf16[512,1024]{0,1:T(8,128)(2,1)S(1)}) fusion(bf16[2048,1024]{0,1:T(8,128)(2,1)} %get-tuple-element.375, s32[]{:T(128)S(6)} %select_n.100, bf16[2048,1024]{0,1:T(8,128)(2,1)} %get-tuple-element.370), kind=kLoop, calls=%fused_computation.10 | loop fusion | bytes 4194308 | tf_op jit(solution)/shard_map/while/body/eval_jaxpr/dynamic_slice | solution.py:64
  161.8 2.7 %fusion = (f32[8,8,128]{2,1,0:T(8,128)S(1)}, f32[8,512,128,8]{2,1,3,0:T(8,128)S(1)}) fusion(pred[128,512]{0,1:T(8,128)(4,1)S(1)} %get-tuple-element.369, bf16[512,8,128,1]{0,2,3,1:T(8,128)(2,1)S(1)} %bitcast.36, bf16[128,8,8,128]{3,0,2,1:T(8,128)(2,1)S(1)} %copy-done), kind=kOutput, calls=%fused_computation.2 | convolution fusion | flops 1086316544 | bytes 20021248 | tf_op jit(solution)/shard_map/while/body/eval_jaxpr/cond/branch_1_fun/rkgd,pkd->kgrp/dot_general | solution.py:29
  164.5 4.2 %fusion.2 = f32[8,8,128]{2,1,0:T(8,128)S(1)} fusion(f32[8,512,128,8]{2,1,3,0:T(8,128)S(1)} %get-tuple-element.444, f32[8,8,128]{2,1,0:T(8,128)S(1)} %max.5, pred[128,512]{0,1:T(8,128)(4,1)S(1)} %get-tuple-element.369), kind=kLoop, calls=%fused_computation.4 | loop fusion | flops 20963328 | bytes 16908288 | tf_op jit(solution)/shard_map/while/body/eval_jaxpr/cond/branch_1_fun/reduce_sum | solution.py:36
  168.8 8.9 %multiply_add_fusion = f32[8,8,128,128]{3,2,1,0:T(8,128)} fusion(f32[8,8,128,128]{3,2,1,0:T(8,128)} %get-tuple-element.374, f32[8,8,128]{2,1,0:T(8,128)S(1)} %get-tuple-element.440, bf16[512,8,128,1]{0,2,3,1:T(8,128)(2,1)} %bitcast.37, f32[8,512,128,8]{2,1,3,0:T(8,128)S(1)} %get-tuple-element.444, f32[8,8,128]{2,1,0:T(8,128)S(1)} %max.5, ...), kind=kOutput, calls=%fused_computation.7 | convolution fusion | flops 1096810496 | bytes 26345472 | tf_op jit(solution)/shard_map/while/body/eval_jaxpr/cond/branch_1_fun/kgrp,pkd->kgrd/dot_general | solution.py:37
  177.7 0.1 select_reduce_fusion.3
  177.8 0.1 convert_reduce_fusion.3
  177.9 0.9 fusion.24
  179.4 18.8 %conditional.2 = ((f32[8,8,128]{2,1,0:T(8,128)S(1)}, f32[8,8,128]{2,1,0:T(8,128)S(1)}, f32[8,8,128,128]{3,2,1,0:T(8,128)})) conditional(s32[]{:T(128)} %convert_element_type.54, (f32[8,8,128]{2,1,0:T(8,128)S(1)}, f32[8,8,128]{2,1,0:T(8,128)S(1)}, f32[8,8,128,128]{3,2,1,0:T(8,128)}) %tuple.62, (pred[128,512]{0,1:T(8,128)(4,1)S(1)}, s32[]{:T(128)}, ...), branch_computations={%region_7.7_spmd, %region_8.10_spmd} | conditional | flops 2204123136 | bytes 76218464 | solution.py:48
  179.4 2.9 %constant_dynamic-slice_fusion = (bf16[512,1024]{0,1:T(8,128)(2,1)}, bf16[512,1024]{0,1:T(8,128)(2,1)S(1)}) fusion(bf16[2048,1024]{0,1:T(8,128)(2,1)} %get-tuple-element.375, s32[]{:T(128)S(6)} %select_n.100, bf16[2048,1024]{0,1:T(8,128)(2,1)} %get-tuple-element.370), kind=kLoop, calls=%fused_computation.10 | loop fusion | bytes 4194308 | tf_op jit(solution)/shard_map/while/body/eval_jaxpr/dynamic_slice | solution.py:64
  182.3 2.7 %fusion = (f32[8,8,128]{2,1,0:T(8,128)S(1)}, f32[8,512,128,8]{2,1,3,0:T(8,128)S(1)}) fusion(pred[128,512]{0,1:T(8,128)(4,1)S(1)} %get-tuple-element.369, bf16[512,8,128,1]{0,2,3,1:T(8,128)(2,1)S(1)} %bitcast.36, bf16[128,8,8,128]{3,0,2,1:T(8,128)(2,1)S(1)} %copy-done), kind=kOutput, calls=%fused_computation.2 | convolution fusion | flops 1086316544 | bytes 20021248 | tf_op jit(solution)/shard_map/while/body/eval_jaxpr/cond/branch_1_fun/rkgd,pkd->kgrp/dot_general | solution.py:29
  185.0 4.2 %fusion.2 = f32[8,8,128]{2,1,0:T(8,128)S(1)} fusion(f32[8,512,128,8]{2,1,3,0:T(8,128)S(1)} %get-tuple-element.444, f32[8,8,128]{2,1,0:T(8,128)S(1)} %max.5, pred[128,512]{0,1:T(8,128)(4,1)S(1)} %get-tuple-element.369), kind=kLoop, calls=%fused_computation.4 | loop fusion | flops 20963328 | bytes 16908288 | tf_op jit(solution)/shard_map/while/body/eval_jaxpr/cond/branch_1_fun/reduce_sum | solution.py:36
  189.3 8.9 %multiply_add_fusion = f32[8,8,128,128]{3,2,1,0:T(8,128)} fusion(f32[8,8,128,128]{3,2,1,0:T(8,128)} %get-tuple-element.374, f32[8,8,128]{2,1,0:T(8,128)S(1)} %get-tuple-element.440, bf16[512,8,128,1]{0,2,3,1:T(8,128)(2,1)} %bitcast.37, f32[8,512,128,8]{2,1,3,0:T(8,128)S(1)} %get-tuple-element.444, f32[8,8,128]{2,1,0:T(8,128)S(1)} %max.5, ...), kind=kOutput, calls=%fused_computation.7 | convolution fusion | flops 1096810496 | bytes 26345472 | tf_op jit(solution)/shard_map/while/body/eval_jaxpr/cond/branch_1_fun/kgrp,pkd->kgrd/dot_general | solution.py:37
  198.2 2.9 %fusion.15 = bf16[128,8,8,128]{3,0,2,1:T(8,128)(2,1)S(1)} fusion(f32[8,8,128,128]{3,2,1,0:T(8,128)} %get-tuple-element.393, f32[8,8,128]{2,1,0:T(8,128)S(1)} %get-tuple-element.394), kind=kLoop, calls=%fused_computation.32 | loop fusion | flops 2097152 | bytes 6324224 | tf_op jit(solution)/shard_map/convert_element_type | solution.py:100
  201.1 1.4 copy.23
  202.5 3.1 %copy.33 = bf16[16,8,64,128]{3,1,2,0:T(8,128)(2,1)} copy(bf16[16,8,64,128]{3,2,1,0:T(8,128)(2,1)S(1)} %bitcast.38) | data formatting | bytes 4194304
  (38 shorter events, 0.3 us)
Async XLA Ops:
  6.5 54.4 %all-gather.3.cloned.1.call-start = ((), (), s32[]{:S(2)}) async-start(), calls=%async_computation | async-start | bytes 4456448 | tf_op jit(solution)/shard_map/all_gather | solution.py:113
  8.4 105.4 %all-gather.5.cloned.1.call-start = ((), (), s32[]{:S(2)}) async-start(), calls=%async_computation.1 | async-start | bytes 4456448 | tf_op jit(solution)/shard_map/all_gather | solution.py:114
  10.2 5.9 %copy-start.2 = (s32[4]{0:T(128)S(1)}, s32[4]{0:T(128)}, u32[]{:S(2)}) copy-start(s32[4]{0:T(128)} %param.12) | copy-start | bytes 52
  10.2 6.0 %copy-start.1 = (s32[16]{0:T(128)S(1)}, s32[16]{0:T(128)}, u32[]{:S(2)}) copy-start(s32[16]{0:T(128)} %param.13) | copy-start | bytes 196
  117.9 2.9 %copy-start = (bf16[128,8,8,128]{3,0,2,1:T(8,128)(2,1)S(1)}, bf16[128,8,8,128]{3,0,2,1:T(8,128)(2,1)}, u32[]{:S(2)}) copy-start(bf16[128,8,8,128]{3,0,2,1:T(8,128)(2,1)} %get-tuple-element.372) | copy-start | bytes 6291460 | tf_op jit(solution)/shard_map/while/body/eval_jaxpr/cond
  138.4 2.9 %copy-start = (bf16[128,8,8,128]{3,0,2,1:T(8,128)(2,1)S(1)}, bf16[128,8,8,128]{3,0,2,1:T(8,128)(2,1)}, u32[]{:S(2)}) copy-start(bf16[128,8,8,128]{3,0,2,1:T(8,128)(2,1)} %get-tuple-element.372) | copy-start | bytes 6291460 | tf_op jit(solution)/shard_map/while/body/eval_jaxpr/cond
  158.9 2.9 %copy-start = (bf16[128,8,8,128]{3,0,2,1:T(8,128)(2,1)S(1)}, bf16[128,8,8,128]{3,0,2,1:T(8,128)(2,1)}, u32[]{:S(2)}) copy-start(bf16[128,8,8,128]{3,0,2,1:T(8,128)(2,1)} %get-tuple-element.372) | copy-start | bytes 6291460 | tf_op jit(solution)/shard_map/while/body/eval_jaxpr/cond
  179.4 2.9 %copy-start = (bf16[128,8,8,128]{3,0,2,1:T(8,128)(2,1)S(1)}, bf16[128,8,8,128]{3,0,2,1:T(8,128)(2,1)}, u32[]{:S(2)}) copy-start(bf16[128,8,8,128]{3,0,2,1:T(8,128)(2,1)} %get-tuple-element.372) | copy-start | bytes 6291460 | tf_op jit(solution)/shard_map/while/body/eval_jaxpr/cond
Sparse Core Ops, SparseCore 0:
  9.5 51.3 all-gather.2
  63.0 50.6 all-gather.4
where the time goes:
time: 216 us; the launch traced here: 212 us
  waiting for transfers between devices  97.3 us (45%)
  matrix products  46.3 us (21%)
  local copies, waits for them, and re-layouts  28 us (13%)
  other arithmetic  24.6 us (11%)
  between operations  13.5 us (6%)
  loops' own time  2.71 us (1%)
    all_gather x1, waiting for transfers between devices, local(): lax.all_gather(values, ('seq', 'head'), axis=0, tiled=True)  52.8 us
    all_gather x1, waiting for transfers between devices, local(): lax.all_gather(keys, ('seq', 'head'), axis=0, tiled=True)  44.4 us
    dot_general x4, matrix products, compute(): jnp.einsum('kgrp,pkd->kgrd', weights.astype(jnp.bfloat16), value_block, p...  35.6 us
    reduce_sum x4, other arithmetic, compute(): total = total * factor + jnp.sum(weights, axis=-1)  17 us
    dynamic_slice x4, local copies, waits for them, and re-layouts, advance(): lax.dynamic_slice_in_dim(value_rows, offset, width, 0)  11.6 us
    dot_general x4, matrix products, compute(): jnp.einsum('rkgd,pkd->kgrp', grouped, key_block, preferred_element_type=j...  10.7 us
    unnamed x8, local copies, waits for them, and re-layouts  9.95 us
  transfers between devices with their start and end apart: 2, of which 2 were waited for; matrix products, arithmetic and copies ran while one was open for 4% of the time, Pallas kernels for 0%

commit v1 on v0

v1 whole, which is shorter than its diff:
```python
import functools
import math

import jax
import jax.numpy as jnp
from jax import lax
from jax.experimental import pallas as pl
from jax.experimental.pallas import tpu as pltpu
from jax.sharding import PartitionSpec as P

QUERY_HEADS = 64
KEY_VALUE_HEADS = 8
HEAD_SIZE = 128
QUERY_GROUP = QUERY_HEADS // KEY_VALUE_HEADS
MESH = pl.DeviceIdType.MESH


def ring_pos(chip, chips):
    odd = chip % 2
    return (1 - odd) * (chip // 2) + odd * ((2 * chips - 1 - chip) // 2)


def ring_chip(pos, chips):
    back = pos // (chips // 2)
    return (1 - back) * (2 * pos) + back * (2 * chips - 1 - 2 * pos)


def kernel(chips, window, docs, lengths, assign, q_hbm, k_hbm, v_hbm, out, *scratch):
    heads = KEY_VALUE_HEADS // 2
    mine = scratch[:heads]
    sib = scratch[heads : 2 * heads]
    (queries, k_win, v_win, bias, q_sem, own_sem, ring_recv, ring_send,
     sib_recv, sib_send, swap_send) = scratch[2 * heads :]
    span = queries.shape[0]
    half = chips // 2
    group = lax.axis_index("group")
    chip = lax.axis_index("seq")
    core = lax.axis_index("head")
    pos = ring_pos(chip, chips)
    other = 1 - core

    def device(p):
        return (group, ring_chip(p, chips), core)

    right = device((pos + 1) % chips)
    left = device((pos + chips - 1) % chips)
    twin = (group, chip, other)

    barrier = pltpu.get_barrier_semaphore()
    for target in (right, left, twin):
        pl.semaphore_signal(barrier, inc=1, device_id=target, device_id_type=MESH)

    def columns(index):
        return pl.ds(pl.multiple_of(index * HEAD_SIZE, HEAD_SIZE), HEAD_SIZE)

    for h in range(heads):
        for part, array in enumerate((k_hbm, v_hbm)):
            pltpu.make_async_copy(
                array.at[:, columns(core * heads + h)],
                mine[h].at[pos, part, core],
                own_sem.at[h],
            ).start()
    q_copy = pltpu.make_async_copy(q_hbm, queries, q_sem)
    pl.semaphore_wait(barrier, 3)
    for h in range(heads):
        for part, array in enumerate((k_hbm, v_hbm)):
            pltpu.make_async_remote_copy(
                array.at[:, columns(other * heads + h)],
                mine[h].at[pos, part, core],
                swap_send.at[h],
                own_sem.at[h],
                device_id=twin,
                device_id_type=MESH,
            ).start()
    q_copy.start()

    def ring_copy(h, way, step, part):
        block = (pos + chips - step + 1) % chips if way == 0 else (pos + step - 1) % chips
        return pltpu.make_async_remote_copy(
            mine[h].at[block, part],
            mine[h].at[block, part],
            ring_send.at[h],
            ring_recv.at[h, way, 2 * (step - 1) + part],
            device_id=right if way == 0 else left,
            device_id_type=MESH,
        )

    def send_own(h):
        pltpu.make_async_copy(mine[h].at[pos], mine[h].at[pos], own_sem.at[h]).wait()
        for part in range(2):
            for way in range(2):
                ring_copy(h, way, 1, part).start()

    def share(h, block, part):
        pltpu.make_async_remote_copy(
            mine[h].at[block, part],
            sib[h].at[block, part],
            sib_send.at[h],
            sib_recv.at[h],
            device_id=twin,
            device_id_type=MESH,
        ).start()

    def share_own(h):
        for part in range(2):
            share(h, pos, part)

    send_own(0)
    send_own(1)
    share_own(0)
    share_own(1)

    me = chip * 2 + core
    place = assign[me]
    slots = []
    for j in range(window):
        wanted = jnp.maximum(place - j, 0)
        found = jnp.int32(0)
        for r in range(2 * chips):
            slot = ring_pos(r // 2, chips) * 2 + r % 2
            found = found + jnp.where(assign[r] == wanted, slot, 0)
        slots.append(jnp.minimum(found, 2 * chips - 1))

    row = place * span + lax.broadcasted_iota(jnp.int32, (span, 1), 0)
    opened = jnp.zeros((span, 1), jnp.int32)
    end = jnp.int32(0)
    for d in range(docs):
        end = end + lengths[d]
        opened = jnp.where(row >= end, end, opened)
    for j in range(window):
        column = (place - j) * span + lax.broadcasted_iota(jnp.int32, (span, span), 1)
        seen = (column >= opened) & (column <= row)
        bias[:, j * span : (j + 1) * span] = jnp.where(seen, 0.0, -1e30)

    q_copy.wait()
    per = max(1, 2 * QUERY_GROUP // chips)
    chunks = QUERY_GROUP // per
    factor = math.log2(math.e) / math.sqrt(HEAD_SIZE)

    def take(buffer):
        for j in range(window):
            k_win[j * span : (j + 1) * span, :] = buffer[slots[j] // 2, 0, slots[j] % 2]
            v_win[j * span : (j + 1) * span, :] = buffer[slots[j] // 2, 1, slots[j] % 2]

    def attend(key_head, chunk):
        first = key_head * QUERY_GROUP + chunk * per
        stacked = jnp.concatenate([queries[:, columns(first + i)] for i in range(per)], axis=0)
        scores = lax.dot_general(
            stacked, k_win[...], (((1,), (1,)), ((), ())), preferred_element_type=jnp.float32
        )
        shade = bias[...]
        scores = scores * factor + jnp.concatenate([shade] * per, axis=0)
        top = jnp.max(scores, axis=1, keepdims=True)
        weights = jnp.exp2(scores - top)
        total = jnp.sum(weights, axis=1, keepdims=True)
        result = jnp.dot(
            weights.astype(jnp.bfloat16), v_win[...], preferred_element_type=jnp.float32
        )
        result = (result / total).astype(out.dtype)
        for i in range(per):
            out[:, columns(first + i)] = result[i * span : (i + 1) * span]

    def whole(buffer, sem):
        pltpu.make_async_copy(buffer, buffer, sem).wait()

    for h in range(heads + 1):
        if h < heads and h >= 1 and h + 1 < heads:
            send_own(h + 1)
            share_own(h + 1)
        if h >= 1:
            take(mine[h - 1])

        def turn(i, carry, h=h):
            if h < heads:
                step = i // 2 + 1
                part = i % 2
                for way in range(2):
                    def arrive(way=way):
                        came = (pos + chips - step) % chips if way == 0 else (pos + step) % chips
                        ring_copy(h, way, step, part).wait_recv()

                        @pl.when(i < chips - 4 + 1 if way == 0 else i < chips - 4)
                        def _():
                            ring_copy(h, way, step + 1, part).start()

                        if way == 1:
                            @pl.when(i == chips - 3)
                            def _():
                                ring_copy(h, way, step + 1, part).start()

                        share(h, came, part)

                    if way == 0:
                        pl.when(i < chips - 1)(arrive)
                    else:
                        pl.when((i < chips - 2) | (i == chips - 1))(arrive)
            if h >= 1:
                @pl.when(i == chunks)
                def _():
                    whole(sib[h - 1], sib_recv.at[h - 1])
                    take(sib[h - 1])

                twin_turn = i // chunks
                owner = (1 - twin_turn) * core + twin_turn * other
                attend(owner * heads + h - 1, i % chunks)
            return carry

        lax.fori_loop(0, chips, turn, 0)

    for h in range(heads):
        rest = mine[h].at[pl.ds(0, chips - 1)]
        pltpu.make_async_copy(rest, rest, ring_send.at[h]).wait()
        whole(mine[h], sib_send.at[h])
        swapped = mine[h].at[0, 0]
        pltpu.make_async_copy(swapped, swapped, swap_send.at[h]).wait()


def local(chips, queries, keys, values, lengths, assign):
    span = queries.shape[0]
    heads = KEY_VALUE_HEADS // 2
    window = assign.shape[0] // 2 + 1
    docs = lengths.shape[0]
    buffers = [
        pltpu.VMEM((chips, 2, 2, span, HEAD_SIZE), jnp.bfloat16) for _ in range(2 * heads)
    ]
    smem = pl.BlockSpec(memory_space=pltpu.SMEM)
    anywhere = pl.BlockSpec(memory_space=pl.ANY)
    dma = pltpu.SemaphoreType.DMA
    return pl.pallas_call(
        functools.partial(kernel, chips, window, docs),
        out_shape=jax.ShapeDtypeStruct(queries.shape, queries.dtype),
        in_specs=[smem, smem, anywhere, anywhere, anywhere],
        out_specs=pl.BlockSpec(memory_space=pltpu.VMEM),
        scratch_shapes=[
            *buffers,
            pltpu.VMEM(queries.shape, queries.dtype),
            pltpu.VMEM((window * span, HEAD_SIZE), jnp.bfloat16),
            pltpu.VMEM((window * span, HEAD_SIZE), jnp.bfloat16),
            pltpu.VMEM((span, window * span), jnp.float32),
            dma(()),
            dma((heads,)),
            dma((heads, 2, chips)),
            dma((heads,)),
            dma((heads,)),
            dma((heads,)),
            dma((heads,)),
        ],
        compiler_params=pltpu.CompilerParams(
            collective_id=0, has_side_effects=True, vmem_limit_bytes=60 * 1024 * 1024
        ),
    )(lengths, assign, queries, keys, values)


def solution(mesh):
    rows = P(("group", "seq", "head"), None)
    return jax.shard_map(
        functools.partial(local, mesh.shape["seq"]),
        mesh=mesh,
        in_specs=(rows, rows, rows, P("group"), P("group")),
        out_specs=rows,
        check_vma=False,
    )
```

time: 216 us -> 78.7 us (0.36)
  the two profiles are of different devices: /device:TPU:13 before, /device:TPU:0 now
where the time goes in v1:
time: 78.7 us; the launch traced here: 78.5 us
  Pallas kernels  75.4 us (96%)
  local copies, waits for them, and re-layouts  3.1 us (4%)
    pallas_call x1, Pallas kernels, local(): pl.pallas_call(functools.partial(kernel, chips, window, docs), out_shape=...  75.4 us
    unnamed x1, local copies, waits for them, and re-layouts  3.1 us

profile of v1, /device:TPU:0, one launch (start us, length us, event | category | flops | bytes accessed | tf_op | source)
XLA Modules:
  0.0 78.5 jit_solution(8930156621610114830)
XLA Ops:
  0.0 75.4 %shard_map.55 = bf16[128,8192]{1,0:T(8,128)(2,1)} custom-call(s32[4]{0:T(128)} %lengths.1, s32[16]{0:T(128)} %assign.1, bf16[128,8192]{1,0:T(8,128)(2,1)} %q_hbm.1, bf16[128,1024]{1,0:T(8,128)(2,1)} %k_hbm.1, bf16[128,1024]{1,0:T(8,128)(2,1)} %v_hbm.1), custom_call_target="tpu_custom_call" | custom-call | tf_op jit(solution)/shard_map/pallas_call | solution.py:229
  75.4 3.1 %copy.7 = bf16[128,8192]{1,0:T(8,128)(2,1)} copy(bf16[128,8192]{1,0:T(8,128)(2,1)} %shard_map.55) | data formatting | bytes 4194304

commit v2 on v1

--- a/solution.py
+++ b/solution.py
@@ -74,13 +74,13 @@
             ).start()
     q_copy.start()
 
-    def ring_copy(h, way, step, part):
+    def ring_copy(h, way, step, part, piece):
         block = (pos + chips - step + 1) % chips if way == 0 else (pos + step - 1) % chips
         return pltpu.make_async_remote_copy(
-            mine[h].at[block, part],
-            mine[h].at[block, part],
+            mine[h].at[block, part, piece],
+            mine[h].at[block, part, piece],
             ring_send.at[h],
-            ring_recv.at[h, way, 2 * (step - 1) + part],
+            ring_recv.at[h, way, 4 * (step - 1) + 2 * part + piece],
             device_id=right if way == 0 else left,
             device_id_type=MESH,
         )
@@ -88,13 +88,14 @@
     def send_own(h):
         pltpu.make_async_copy(mine[h].at[pos], mine[h].at[pos], own_sem.at[h]).wait()
         for part in range(2):
-            for way in range(2):
-                ring_copy(h, way, 1, part).start()
-
-    def share(h, block, part):
+            for piece in range(2):
+                for way in range(2):
+                    ring_copy(h, way, 1, part, piece).start()
+
+    def share(h, block, part, piece):
         pltpu.make_async_remote_copy(
-            mine[h].at[block, part],
-            sib[h].at[block, part],
+            mine[h].at[block, part, piece],
+            sib[h].at[block, part, piece],
             sib_send.at[h],
             sib_recv.at[h],
             device_id=twin,
@@ -103,7 +104,8 @@
 
     def share_own(h):
         for part in range(2):
-            share(h, pos, part)
+            for piece in range(2):
+                share(h, pos, part, piece)
 
     send_own(0)
     send_own(1)
@@ -133,79 +135,83 @@
         bias[:, j * span : (j + 1) * span] = jnp.where(seen, 0.0, -1e30)
 
     q_copy.wait()
-    per = max(1, 2 * QUERY_GROUP // chips)
-    chunks = QUERY_GROUP // per
+    turns = chips // 2
+    per = QUERY_GROUP // turns
     factor = math.log2(math.e) / math.sqrt(HEAD_SIZE)
 
-    def take(buffer):
+    def take(buffer, place_of):
         for j in range(window):
-            k_win[j * span : (j + 1) * span, :] = buffer[slots[j] // 2, 0, slots[j] % 2]
-            v_win[j * span : (j + 1) * span, :] = buffer[slots[j] // 2, 1, slots[j] % 2]
-
-    def attend(key_head, chunk):
-        first = key_head * QUERY_GROUP + chunk * per
-        stacked = jnp.concatenate([queries[:, columns(first + i)] for i in range(per)], axis=0)
-        scores = lax.dot_general(
-            stacked, k_win[...], (((1,), (1,)), ((), ())), preferred_element_type=jnp.float32
-        )
-        shade = bias[...]
-        scores = scores * factor + jnp.concatenate([shade] * per, axis=0)
-        top = jnp.max(scores, axis=1, keepdims=True)
-        weights = jnp.exp2(scores - top)
-        total = jnp.sum(weights, axis=1, keepdims=True)
-        result = jnp.dot(
-            weights.astype(jnp.bfloat16), v_win[...], preferred_element_type=jnp.float32
-        )
-        result = (result / total).astype(out.dtype)
-        for i in range(per):
-            out[:, columns(first + i)] = result[i * span : (i + 1) * span]
+            at = slice(j * span, (j + 1) * span)
+            k_win[place_of, at, :] = buffer[slots[j] // 2, 0, slots[j] % 2]
+            v_win[place_of, at, :] = buffer[slots[j] // 2, 1, slots[j] % 2]
+
+    def attend(h, chunk):
+        starts = [(owner * heads + h) * QUERY_GROUP + chunk * per for owner in (core, other)]
+        shade = jnp.concatenate([bias[...]] * per, axis=0)
+        results = []
+        for place_of, first in enumerate(starts):
+            stacked = jnp.concatenate([queries[:, columns(first + i)] for i in range(per)], axis=0)
+            scores = lax.dot_general(
+                stacked, k_win[place_of], (((1,), (1,)), ((), ())),
+                preferred_element_type=jnp.float32,
+            )
+            scores = scores * factor + shade
+            top = jnp.max(scores, axis=1, keepdims=True)
+            weights = jnp.exp2(scores - top)
+            total = jnp.sum(weights, axis=1, keepdims=True)
+            result = jnp.dot(
+                weights.astype(jnp.bfloat16), v_win[place_of], preferred_element_type=jnp.float32
+            )
+            results.append((result / total).astype(out.dtype))
+        for first, result in zip(starts, results):
+            for i in range(per):
+                out[:, columns(first + i)] = result[i * span : (i + 1) * span]
 
     def whole(buffer, sem):
         pltpu.make_async_copy(buffer, buffer, sem).wait()
 
-    for h in range(heads + 1):
-        if h < heads and h >= 1 and h + 1 < heads:
-            send_own(h + 1)
-            share_own(h + 1)
-        if h >= 1:
-            take(mine[h - 1])
-
-        def turn(i, carry, h=h):
-            if h < heads:
-                step = i // 2 + 1
-                part = i % 2
-                for way in range(2):
-                    def arrive(way=way):
-                        came = (pos + chips - step) % chips if way == 0 else (pos + step) % chips
-                        ring_copy(h, way, step, part).wait_recv()
-
-                        @pl.when(i < chips - 4 + 1 if way == 0 else i < chips - 4)
-                        def _():
-                            ring_copy(h, way, step + 1, part).start()
-
-                        if way == 1:
-                            @pl.when(i == chips - 3)
-                            def _():
-                                ring_copy(h, way, step + 1, part).start()
-
-                        share(h, came, part)
-
-                    if way == 0:
-                        pl.when(i < chips - 1)(arrive)
-                    else:
-                        pl.when((i < chips - 2) | (i == chips - 1))(arrive)
-            if h >= 1:
-                @pl.when(i == chunks)
+    def relay(h, i):
+        step = i // 2 + 1
+        part = i % 2
+
+        def arrive(way, piece):
+            came = (pos + chips - step) % chips if way == 0 else (pos + step) % chips
+            ring_copy(h, way, step, part, piece).wait_recv()
+            onward = i < chips - 3 if way == 0 else (i < chips - 4) | (i == chips - 3)
+
+            @pl.when(onward)
+            def _():
+                ring_copy(h, way, step + 1, part, piece).start()
+
+            share(h, came, part, piece)
+
+        for piece in range(2):
+            pl.when(i < chips - 1)(functools.partial(arrive, 0, piece))
+            pl.when((i < chips - 2) | (i == chips - 1))(functools.partial(arrive, 1, piece))
+
+    for phase in range(heads + 2):
+
+        def turn(i, carry, phase=phase):
+            if 1 <= phase <= heads:
+                relay(phase - 1, i + turns)
+            if phase < heads:
+                relay(phase, i)
+            if phase + 2 < heads:
+                @pl.when(i == turns // 2)
                 def _():
-                    whole(sib[h - 1], sib_recv.at[h - 1])
-                    take(sib[h - 1])
-
-                twin_turn = i // chunks
-                owner = (1 - twin_turn) * core + twin_turn * other
-                attend(owner * heads + h - 1, i % chunks)
+                    send_own(phase + 2)
+                    share_own(phase + 2)
+            if phase >= 2:
+                @pl.when(i == 0)
+                def _():
+                    take(mine[phase - 2], 0)
+                    whole(sib[phase - 2], sib_recv.at[phase - 2])
+                    take(sib[phase - 2], 1)
+
+                attend(phase - 2, i)
             return carry
 
-        lax.fori_loop(0, chips, turn, 0)
+        lax.fori_loop(0, turns, turn, 0)
 
     for h in range(heads):
         rest = mine[h].at[pl.ds(0, chips - 1)]
@@ -234,12 +240,12 @@
         scratch_shapes=[
             *buffers,
             pltpu.VMEM(queries.shape, queries.dtype),
-            pltpu.VMEM((window * span, HEAD_SIZE), jnp.bfloat16),
-            pltpu.VMEM((window * span, HEAD_SIZE), jnp.bfloat16),
+            pltpu.VMEM((2, window * span, HEAD_SIZE), jnp.bfloat16),
+            pltpu.VMEM((2, window * span, HEAD_SIZE), jnp.bfloat16),
             pltpu.VMEM((span, window * span), jnp.float32),
             dma(()),
             dma((heads,)),
-            dma((heads, 2, chips)),
+            dma((heads, 2, 2 * chips)),
             dma((heads,)),
             dma((heads,)),
             dma((heads,)),

time: 78.7 us -> 65.1 us (0.83)
  Pallas kernels: 75.4 us -> 61.8 us
    pallas_call x1, Pallas kernels: 75.4 us -> 61.8 us  [local(): pl.pallas_call(functools.partial(kernel, chips, window, docs), out_shape=...]
where the time goes in v2:
time: 65.1 us; the launch traced here: 64.9 us
  Pallas kernels  61.8 us (95%)
  local copies, waits for them, and re-layouts  3.1 us (5%)
    pallas_call x1, Pallas kernels, local(): pl.pallas_call(functools.partial(kernel, chips, window, docs), out_shape=...  61.8 us
    unnamed x1, local copies, waits for them, and re-layouts  3.1 us

profile of v2, /device:TPU:0, one launch (start us, length us, event | category | flops | bytes accessed | tf_op | source)
XLA Modules:
  0.0 64.9 jit_solution(15305613122087886274)
XLA Ops:
  0.0 61.8 %shard_map.55 = bf16[128,8192]{1,0:T(8,128)(2,1)} custom-call(s32[4]{0:T(128)} %lengths.1, s32[16]{0:T(128)} %assign.1, bf16[128,8192]{1,0:T(8,128)(2,1)} %q_hbm.1, bf16[128,1024]{1,0:T(8,128)(2,1)} %k_hbm.1, bf16[128,1024]{1,0:T(8,128)(2,1)} %v_hbm.1), custom_call_target="tpu_custom_call" | custom-call | tf_op jit(solution)/shard_map/pallas_call | solution.py:235
  61.8 3.1 %copy.7 = bf16[128,8192]{1,0:T(8,128)(2,1)} copy(bf16[128,8192]{1,0:T(8,128)(2,1)} %shard_map.55) | data formatting | bytes 4194304
